TPU v7x, 32 devices: a whole 2x2x4 slice. The times are simulated.
32 devices in a mesh: ctx: 8 (over y, x, core), tp: 4 (over z).
Axes of the slice: x: 2, y: 2, z: 4, core: 2. Of those that a mesh axis runs over, the one named last changes fastest.
Arguments:
- hidden: bfloat16 [2048, 8192], P('ctx', 'tp'), may hold values from -6 to 6
- queries: bfloat16 [2048, 4096], P('ctx', 'tp'), may hold values from -1000 to 1000
- kv_weight: bfloat16 [8192, 1024], P('tp', 'ctx'), may hold values from -0.0625 to 0.0625
- kv_bias: bfloat16 [1024], P('tp'), may hold values from -3 to 3
- window: int32 [4], P('tp'), may hold values from 1024 to 4096, as said below
- segment_ids: int32 [2048], P('ctx'), may hold values from 0 to 3, never falling along the last dimension, each value on 1 to 1024 neighbouring positions
Outputs:
- attended: bfloat16 [2048, 4096], P('ctx', 'tp')
- kv_cache: bfloat16 [2048, 1024], P('ctx', 'tp')
Inputs may be any that keep to these rules, and one draw needn't show every extreme that they name: `window`: each entry is 1024 to 4096; some key head's entry equals 4096.
All inputs are finite; a program needn't handle non-finite values.
Results may differ from a plain program's by a relative error of at most 0.012.
Values may be sent and summed in bfloat16 or wider, within the bound.
A program may use at most 64 MiB of HBM per device.

v0:
```python
import functools

import jax
import jax.numpy as jnp
import numpy as np
from jax import lax
from jax.experimental import pallas as pl
from jax.experimental.pallas import tpu as pltpu
from jax.sharding import PartitionSpec as P

WINDOW = 4096
MESH = pl.DeviceIdType.MESH
LOG2E = 1.4426950408889634


rope_base = 1000000.0


def passed_along(value, axis, steps):
    count = lax.axis_size(axis)
    initial, last = (max(0, -steps), min(count, count - steps))
    return lax.ppermute(value, axis, [(source, source + steps) for source in range(initial, last)])


def rotate(values, positions):
    half = values.shape[-1] // 2
    freqs = rope_base ** (-2.0 * jnp.arange(half, dtype=jnp.float32) / values.shape[-1])
    angles = positions.astype(jnp.float32)[:, None] * freqs[None, :]
    cosine = jnp.cos(angles)
    sine = jnp.sin(angles)
    former = values[:, :half]
    latter = values[:, half:]
    return jnp.concatenate(
        [former * cosine - latter * sine, latter * cosine + former * sine], axis=1
    )


def attend(carry, query_rows, query_pos, query_seg, reach, block, block_seg, block_pos):
    running_max, running_sum, weighted = carry
    head = block.shape[1] // 2
    scores = lax.dot_general(
        query_rows, block[:, :head], (((1,), (1,)), ((), ())), preferred_element_type=jnp.float32
    )
    scores = scores * head ** (-0.5)
    gap = query_pos[:, None] - block_pos[None, :]
    allowed = (
        (query_seg[:, None] == block_seg[None, :])
        & (gap >= 0)
        & (gap < reach)
        & (block_pos >= 0)[None, :]
    )
    scores = jnp.where(allowed, scores, -jnp.inf)
    newest = jnp.maximum(running_max, jnp.max(scores, axis=1))
    probs = jnp.exp(scores - newest[:, None])
    rescale = jnp.exp(running_max - newest)
    summed = running_sum * rescale + jnp.sum(probs, axis=1)
    mixed = jnp.dot(probs.astype(jnp.bfloat16), block[:, head:], preferred_element_type=jnp.float32)
    return (newest, summed, weighted * rescale[:, None] + mixed)


def body(hidden, queries, kv_weight, kv_bias, window, segment_ids):
    tok_rows = hidden.shape[0]
    terms = jnp.dot(
        hidden,
        lax.all_gather(kv_weight, "ctx", axis=1, tiled=True),
        preferred_element_type=jnp.float32,
    )
    projected = lax.psum_scatter(terms, "tp", scatter_dimension=1, tiled=True)
    projected = projected + kv_bias.astype(jnp.float32)[None, :]
    head = kv_bias.shape[0] // 2
    shard = lax.axis_index("ctx")
    offsets = jnp.arange(tok_rows, dtype=jnp.int32)
    positions = shard * tok_rows + offsets
    cache = jnp.concatenate(
        [rotate(projected[:, :head], positions), projected[:, head:]], axis=1
    ).astype(jnp.bfloat16)
    group = queries.shape[1] // head
    query_rows = queries.reshape(tok_rows * group, head)
    query_pos = jnp.repeat(positions, group)
    query_seg = jnp.repeat(segment_ids, group)
    reach = window[0]

    def absorb(carry, block, block_seg, block_pos):
        return attend(carry, query_rows, query_pos, query_seg, reach, block, block_seg, block_pos)

    row_count = tok_rows * group
    carry = (
        jnp.full((row_count,), -jnp.inf, jnp.float32),
        jnp.zeros((row_count,), jnp.float32),
        jnp.zeros((row_count, head), jnp.float32),
    )
    carry = absorb(carry, cache, segment_ids, positions)
    halo_count = WINDOW // tok_rows
    held_kv = cache
    held_seg = segment_ids
    have = 0
    while have < halo_count:
        got_kv, got_seg = passed_along((held_kv, held_seg), "ctx", max(have, 1))
        shards = got_kv.shape[0] // tok_rows
        for member in range(shards):
            lower = member * tok_rows
            block_pos = (shard - have - shards + member) * tok_rows + offsets
            carry = absorb(
                carry,
                got_kv[lower : lower + tok_rows],
                got_seg[lower : lower + tok_rows],
                block_pos,
            )
        if have == 0:
            held_kv, held_seg = (got_kv, got_seg)
        else:
            held_kv = jnp.concatenate([got_kv, held_kv], axis=0)
            held_seg = jnp.concatenate([got_seg, held_seg], axis=0)
        have = have + shards
    newest, summed, weighted = carry
    attended = (weighted / summed[:, None]).reshape(tok_rows, group * head).astype(jnp.bfloat16)
    return (attended, cache)


def fused_kernel(
    halo, back, window_ref, hid_hbm, w_hbm, q_hbm, bias_hbm, freq_hbm, seg_hbm, out_ref, cache_ref,
    kv_ref, segs_ref, hbuf, wbuf, part_out, part_in, own, cosb, sinb,
    q_ref, bias_ref, freq_ref, seg_line, seg_ref, mask, probs, totals,
    local_sem, hid_sem, gate, wsend, wrecv, psend, precv, ksend, krecv, fsend, frecv, ssend, srecv,
):
    c = lax.axis_index("ctx")
    t = lax.axis_index("tp")
    n_ctx = lax.axis_size("ctx")
    n_tp = lax.axis_size("tp")
    pairs = n_ctx // 2
    pair = c // 2
    core = c % 2
    mate = pair * 2 + (1 - core)
    toks = hid_hbm.shape[0]
    feats, head = w_hbm.shape
    half = feats // 2
    span = 2 * toks
    own_rows = pl.ds(pl.multiple_of(core * toks, toks), toks)

    load_w = [
        pltpu.make_async_copy(w_hbm.at[pl.ds(q * half, half)], wbuf.at[0, q], local_sem.at[q])
        for q in range(2)
    ]
    load_h = pltpu.make_async_copy(hid_hbm, hbuf.at[own_rows], local_sem.at[2])
    small = [
        pltpu.make_async_copy(src, dst, local_sem.at[3 + at])
        for at, (src, dst) in enumerate(
            [(seg_hbm, seg_line), (bias_hbm, bias_ref), (freq_hbm, freq_ref), (q_hbm, q_ref)]
        )
    ]
    load_w[0].start()
    load_w[1].start()
    load_h.start()
    for copy in small:
        copy.start()

    barrier = pltpu.get_barrier_semaphore()
    for step in range(1, n_ctx):
        pl.semaphore_signal(barrier, inc=1, device_id=((c + step) % n_ctx, t), device_id_type=MESH)
    for step in range(1, n_tp):
        pl.semaphore_signal(barrier, inc=1, device_id=(c, (t + step) % n_tp), device_id_type=MESH)
    pl.semaphore_wait(barrier, n_ctx + n_tp - 2)

    def neighbour(d):
        other_x = 1 - pair % 2 if d % 2 else pair % 2
        other_y = 1 - pair // 2 if d // 2 else pair // 2
        return other_y * 2 + other_x

    def w_copy(src, dst, q, sem, to):
        return pltpu.make_async_remote_copy(
            src_ref=wbuf.at[src, q], dst_ref=wbuf.at[dst, q],
            send_sem=wsend.at[sem], recv_sem=wrecv.at[dst, q],
            device_id=(2 * neighbour(to) + core, t), device_id_type=MESH,
        )

    x_first, x_second = w_copy(0, 1, 0, 0, 1), w_copy(0, 1, 1, 1, 1)
    y_first, y_second = w_copy(0, 2, 1, 2, 2), w_copy(0, 2, 0, 3, 2)
    relay_y, relay_x = w_copy(1, 3, 0, 4, 2), w_copy(2, 3, 1, 5, 1)

    def send_weights():
        x_first.start()
        y_first.start()
        x_second.start()
        y_second.start()

    load_w[0].wait()
    load_w[1].wait()

    @pl.when(core == 0)
    def _():
        send_weights()

    load_h.wait()
    hid = pltpu.make_async_remote_copy(
        src_ref=hbuf.at[own_rows], dst_ref=hbuf.at[own_rows],
        send_sem=hid_sem.at[0], recv_sem=hid_sem.at[1], device_id=(mate, t), device_id_type=MESH,
    )
    hid.start()
    for copy in small:
        copy.wait()
    seg_ref[...] = jnp.broadcast_to(seg_line[...].reshape(1, toks), seg_ref.shape)

    def seg_copy(step, sub):
        at = pl.ds(pl.multiple_of((back - step) * span + core * toks, toks), toks)
        return pltpu.make_async_remote_copy(
            src_ref=seg_ref, dst_ref=segs_ref.at[:, at],
            send_sem=ssend.at[2 * step + sub], recv_sem=srecv.at[2 * step + core],
            device_id=(jnp.minimum(2 * (pair + step) + sub, n_ctx - 1) if step else mate, t),
            device_id_type=MESH,
        )

    for step in range(back + 1):
        if step == 0:
            segs_ref[:, pl.ds(pl.multiple_of(back * span + core * toks, toks), toks)] = seg_ref[...]
            seg_copy(0, 0).start()
        else:
            @pl.when(pair + step < pairs)
            def _():
                seg_copy(step, 0).start()
                seg_copy(step, 1).start()

            @pl.when(pair < step)
            def _():
                rows = slice((back - step) * span, (back - step + 1) * span)
                segs_ref[:, rows] = jnp.full((segs_ref.shape[0], span), -1, jnp.int32)
                kv_ref[:, rows, :] = jnp.zeros((2, span, head), jnp.bfloat16)

    def multiply(d):
        acc = jnp.dot(hbuf[:, :half], wbuf[d, 0], preferred_element_type=jnp.float32)
        return acc + jnp.dot(hbuf[:, half:], wbuf[d, 1], preferred_element_type=jnp.float32)

    def part_copy(d):
        return pltpu.make_async_remote_copy(
            src_ref=part_out.at[d], dst_ref=part_in.at[t],
            send_sem=psend.at[d], recv_sem=precv.at[t],
            device_id=(c, neighbour(d)), device_id_type=MESH,
        )

    def hand_over(d):
        acc = multiply(d)
        part_out[d] = acc.astype(part_out.dtype)

        @pl.when(neighbour(d) == t)
        def _():
            own[...] = acc

        @pl.when(neighbour(d) != t)
        def _():
            part_copy(d).start()

    hid.wait()
    hand_over(0)

    @pl.when(core == 1)
    def _():
        pl.semaphore_wait(gate, 1)
        send_weights()

    x_first.wait_recv()
    relay_y.start()
    y_first.wait_recv()
    relay_x.start()

    angle_rows = (lax.broadcasted_iota(jnp.int32, (span, head), 0) + pair * span).astype(jnp.float32)
    angles = angle_rows * freq_ref[0:1, :]
    is_key = core == 0
    left = lax.broadcasted_iota(jnp.int32, (span, head), 1) < head // 2
    sine = jnp.sin(angles)
    cosb[...] = jnp.where(is_key, jnp.cos(angles), 1.0)
    sinb[...] = jnp.where(is_key, jnp.where(left, -sine, sine), 0.0)

    x_second.wait_recv()
    hand_over(1)
    y_second.wait_recv()
    hand_over(2)

    def seg_arrival(step, sub):
        at = pl.ds(pl.multiple_of((back - step) * span + sub * toks, toks), toks)
        return pltpu.make_async_remote_copy(
            src_ref=seg_ref, dst_ref=segs_ref.at[:, at],
            send_sem=ssend.at[0], recv_sem=srecv.at[2 * step + sub],
            device_id=(mate, t), device_id_type=MESH,
        )

    seg_arrival(0, 1 - core).wait_recv()
    for step in range(1, back + 1):
        @pl.when(pair >= step)
        def _():
            seg_arrival(step, 0).wait_recv()
            seg_arrival(step, 1).wait_recv()

    width = halo + toks
    start = pl.multiple_of((core + 2 * back) * toks - halo, toks)
    here = pl.ds(pl.multiple_of((core + 2 * back) * toks, toks), toks)
    key_seg = segs_ref[0:1, pl.ds(start, width)]
    query_seg = jnp.transpose(jnp.broadcast_to(seg_ref[0:1, :], (head, toks)))[:, 0:1]
    row = lax.broadcasted_iota(jnp.int32, (toks, width), 0)
    column = lax.broadcasted_iota(jnp.int32, (toks, width), 1)
    gap = row + halo - column
    allowed = (
        (query_seg == key_seg) & (gap >= 0) & (gap < window_ref[0]) & (column >= halo - c * toks)
    )
    mask[...] = jnp.where(allowed, 0.0, -jnp.inf)

    relay_y.wait_recv()
    relay_x.wait_recv()
    for copy in (x_first, x_second, y_first, y_second, relay_y, relay_x):
        copy.wait_send()

    @pl.when(core == 0)
    def _():
        pl.semaphore_signal(gate, inc=1, device_id=(mate, t), device_id_type=MESH)

    hand_over(3)

    def kv_copy(kind, src_step, dst_step, send, recv, to):
        return pltpu.make_async_remote_copy(
            src_ref=kv_ref.at[kind, pl.ds((back - src_step) * span, span)],
            dst_ref=kv_ref.at[kind, pl.ds((back - dst_step) * span, span)],
            send_sem=send, recv_sem=recv, device_id=(to, t), device_id_type=MESH,
        )

    def onward(step):
        to = jnp.minimum(2 * (pair + step) + core, n_ctx - 2 + core)
        return kv_copy(core, 0, step, ksend.at[step], krecv.at[step], to)

    def across(step):
        return kv_copy(core, step, step, fsend.at[step], frecv.at[step], mate)

    def crossed(step):
        return kv_copy(1 - core, step, step, fsend.at[step], frecv.at[step], mate)

    def finish(rotated):
        total = own[...] + bias_ref[...].reshape(1, 2 * head)[:, :head].astype(jnp.float32) if rotated else (
            own[...] + bias_ref[...].reshape(1, 2 * head)[:, head:].astype(jnp.float32)
        )
        for step in range(1, n_tp):
            source = (t + step) % n_tp
            pltpu.make_async_remote_copy(
                src_ref=part_out.at[0], dst_ref=part_in.at[source],
                send_sem=psend.at[0], recv_sem=precv.at[source],
                device_id=(c, source), device_id_type=MESH,
            ).wait_recv()
            total = total + part_in[source].astype(jnp.float32)
        if rotated:
            total = total * cosb[...] + pltpu.roll(total, head // 2, 1) * sinb[...]
        kv_ref[0 if rotated else 1, back * span :, :] = total.astype(jnp.bfloat16)
        across(0).start()
        for step in range(1, back + 1):
            @pl.when(pair + step < pairs)
            def _():
                onward(step).start()

    def pass_on():
        for step in range(1, back + 1):
            @pl.when(pair >= step)
            def _():
                onward(step).wait_recv()
                across(step).start()

    def await_crossed():
        crossed(0).wait_recv()
        for step in range(1, back + 1):
            @pl.when(pair >= step)
            def _():
                crossed(step).wait_recv()

    def weigh(lower, upper):
        keys = kv_ref[0, pl.ds(start, width), :]
        scale = head ** (-0.5) * LOG2E

        def one(h):
            lanes = pl.ds(pl.multiple_of(h * head, head), head)
            scores = lax.dot_general(
                q_ref[:, lanes], keys, (((1,), (1,)), ((), ())), preferred_element_type=jnp.float32
            )
            scores = scores + mask[...]
            top = jnp.max(scores, axis=1, keepdims=True)
            weights = jnp.exp2((scores - top) * scale)
            totals[h] = jnp.sum(weights, axis=1, keepdims=True)
            probs[h] = weights.astype(jnp.bfloat16)

        def couple(i, carry):
            one(2 * i)
            one(2 * i + 1)
            return carry

        lax.fori_loop(lower // 2, upper // 2, couple, 0)

    group = q_ref.shape[1] // head
    early = group // 2

    @pl.when(core == 0)
    def _():
        finish(True)
        pass_on()
        weigh(0, group)
        await_crossed()

    @pl.when(core == 1)
    def _():
        await_crossed()
        weigh(0, early)
        finish(False)
        weigh(early, group)
        pass_on()

    values = kv_ref[1, pl.ds(start, width), :]

    def mix(i, carry):
        for h in (2 * i, 2 * i + 1):
            lanes = pl.ds(pl.multiple_of(h * head, head), head)
            mixed = jnp.dot(probs[h], values, preferred_element_type=jnp.float32)
            out_ref[:, lanes] = (mixed / totals[h]).astype(out_ref.dtype)
        return carry

    lax.fori_loop(0, group // 2, mix, 0)
    cache_ref[:, :head] = kv_ref[0, here, :]
    cache_ref[:, head:] = kv_ref[1, here, :]

    for d in range(n_tp):
        @pl.when(neighbour(d) != t)
        def _():
            part_copy(d).wait_send()
    seg_copy(0, 0).wait_send()
    across(0).wait_send()
    for step in range(1, back + 1):
        @pl.when(pair + step < pairs)
        def _():
            seg_copy(step, 0).wait_send()
            seg_copy(step, 1).wait_send()
            onward(step).wait_send()

        @pl.when(pair >= step)
        def _():
            across(step).wait_send()


def fast_body(halo, back, hidden, queries, kv_weight, kv_bias, window, segment_ids):
    toks, feats = hidden.shape
    head = kv_bias.shape[0] // 2
    span = 2 * toks
    group = queries.shape[1] // head
    n_tp = lax.axis_size("tp")
    freqs = rope_base ** (-2.0 * np.arange(head // 2, dtype=np.float64) / head)
    freqs = np.tile(np.concatenate([freqs, freqs])[None, :], (8, 1)).astype(np.float32)
    keys = (back + 1) * span
    vmem = pl.BlockSpec(memory_space=pltpu.VMEM)
    hbm = pl.BlockSpec(memory_space=pl.ANY)
    dma = pltpu.SemaphoreType.DMA
    return pl.pallas_call(
        functools.partial(fused_kernel, halo, back),
        out_shape=(
            jax.ShapeDtypeStruct(queries.shape, jnp.bfloat16),
            jax.ShapeDtypeStruct((toks, 2 * head), jnp.bfloat16),
        ),
        in_specs=[pl.BlockSpec(memory_space=pltpu.SMEM), hbm, hbm, hbm, hbm, hbm, hbm],
        out_specs=(vmem, vmem),
        scratch_shapes=[
            pltpu.VMEM((2, keys, head), jnp.bfloat16),
            pltpu.VMEM((8, keys), jnp.int32),
            pltpu.VMEM((span, feats), jnp.bfloat16),
            pltpu.VMEM((n_tp, 2, feats // 2, head), jnp.bfloat16),
            pltpu.VMEM((n_tp, span, head), jnp.bfloat16),
            pltpu.VMEM((n_tp, span, head), jnp.bfloat16),
            pltpu.VMEM((span, head), jnp.float32),
            pltpu.VMEM((span, head), jnp.float32),
            pltpu.VMEM((span, head), jnp.float32),
            pltpu.VMEM(queries.shape, jnp.bfloat16),
            pltpu.VMEM((2 * head,), jnp.bfloat16),
            pltpu.VMEM((8, head), jnp.float32),
            pltpu.VMEM((toks,), jnp.int32),
            pltpu.VMEM((8, toks), jnp.int32),
            pltpu.VMEM((toks, halo + toks), jnp.float32),
            pltpu.VMEM((group, toks, halo + toks), jnp.bfloat16),
            pltpu.VMEM((group, toks, 1), jnp.float32),
            dma((7,)),
            dma((2,)),
            pltpu.SemaphoreType.REGULAR,
            dma((6,)),
            dma((n_tp, 2)),
            dma((n_tp,)),
            dma((n_tp,)),
            dma((back + 1,)),
            dma((back + 1,)),
            dma((back + 1,)),
            dma((back + 1,)),
            dma((2 * back + 2,)),
            dma((2 * back + 2,)),
        ],
        compiler_params=pltpu.CompilerParams(collective_id=0, has_side_effects=True),
    )(window, hidden, kv_weight, queries, kv_bias, jnp.asarray(freqs), segment_ids)


def solution(mesh):
    in_specs = (P("ctx", "tp"), P("ctx", "tp"), P("tp", "ctx"), P("tp"), P("tp"), P("ctx"))
    out_specs = (P("ctx", "tp"), P("ctx", "tp"))
    n_ctx, n_tp = mesh.shape["ctx"], mesh.shape["tp"]

    def step(hidden, queries, kv_weight, kv_bias, window, segment_ids):
        toks = hidden.shape[0]
        args = (hidden, queries, kv_weight, kv_bias, window, segment_ids)
        if n_ctx != 8 or n_ctx != 2 * n_tp or 2 * kv_weight.shape[1] != kv_bias.shape[0]:
            return body(*args)
        longest = min(WINDOW, n_ctx * toks // 2)
        blocks = -(-(longest - 1) // toks)
        return fast_body(blocks * toks, -(-blocks // 2), *args)

    return jax.shard_map(step, mesh=mesh, in_specs=in_specs, out_specs=out_specs, check_vma=False)
```

profile of v0, /device:TPU:6, one launch (start us, length us, event | category | flops | bytes accessed | tf_op | source)
XLA Modules:
  0.0 44.2 jit_solution(4091838229783393477)
XLA Ops:
  1.3 40.4 %shard_map.86 = (bf16[256,1024]{1,0:T(8,128)(2,1)}, bf16[256,256]{1,0:T(8,128)(2,1)}) custom-call(s32[1]{0:T(128)S(6)} %copy.11.window_ref, bf16[256,2048]{1,0:T(8,128)(2,1)} %hid_hbm.1, bf16[2048,128]{1,0:T(8,128)(2,1)} %w_hbm.1, bf16[256,1024]{1,0:T(8,128)(2,1)} %q_hbm.1, bf16[256]{0:T(256)(128)(2,1)} %bias_hbm.1, f32[8,128]{1,0:T(8,128)} %constant.2.clone.freq_hbm, ...), custom_call_target="tpu_custom_call" | custom-call | tf_op jit(solution)/shard_map/pallas_call | solution.py:451
  41.6 0.0 copy-start
  41.7 1.9 %copy.12 = bf16[256,1024]{1,0:T(8,128)(2,1)} copy(bf16[256,1024]{1,0:T(8,128)(2,1)} %get-tuple-element.4) | data formatting | bytes 1048576
  43.6 0.0 copy-done
  43.6 0.7 %copy.13 = bf16[256,256]{1,0:T(8,128)(2,1)} copy(bf16[256,256]{1,0:T(8,128)(2,1)S(1)} %copy-done) | data formatting | bytes 262144
Async XLA Ops:
  41.6 1.9 %copy-start = (bf16[256,256]{1,0:T(8,128)(2,1)S(1)}, bf16[256,256]{1,0:T(8,128)(2,1)}, u32[]{:S(2)}) copy-start(bf16[256,256]{1,0:T(8,128)(2,1)} %get-tuple-element.5) | copy-start | bytes 393220
where the time goes:
time: 44.4 us; the launch traced here: 44.2 us
  Pallas kernels  40.4 us (91%)
  local copies, waits for them, and re-layouts  2.56 us (6%)
  between operations  1.29 us (3%)
    pallas_call x1, Pallas kernels, fast_body(): pl.pallas_call(functools.partial(fused_kernel, halo, back), out_shape=(ja...  40.4 us
    unnamed x4, local copies, waits for them, and re-layouts  2.56 us

commit v1 on v0

--- a/solution.py
+++ b/solution.py
@@ -270,8 +270,13 @@
     sinb[...] = jnp.where(is_key, jnp.where(left, -sine, sine), 0.0)
 
     x_second.wait_recv()
+    y_second.wait_recv()
+
+    @pl.when(core == 0)
+    def _():
+        pl.semaphore_signal(gate, inc=1, device_id=(mate, t), device_id_type=MESH)
+
     hand_over(1)
-    y_second.wait_recv()
     hand_over(2)
 
     def seg_arrival(step, sub):
@@ -306,10 +311,6 @@
     relay_x.wait_recv()
     for copy in (x_first, x_second, y_first, y_second, relay_y, relay_x):
         copy.wait_send()
-
-    @pl.when(core == 0)
-    def _():
-        pl.semaphore_signal(gate, inc=1, device_id=(mate, t), device_id_type=MESH)
 
     hand_over(3)
 
@@ -451,8 +452,8 @@
     return pl.pallas_call(
         functools.partial(fused_kernel, halo, back),
         out_shape=(
-            jax.ShapeDtypeStruct(queries.shape, jnp.bfloat16),
-            jax.ShapeDtypeStruct((toks, 2 * head), jnp.bfloat16),
+            pltpu.VMEM(queries.shape, jnp.bfloat16),
+            pltpu.VMEM((toks, 2 * head), jnp.bfloat16),
         ),
         in_specs=[pl.BlockSpec(memory_space=pltpu.SMEM), hbm, hbm, hbm, hbm, hbm, hbm],
         out_specs=(vmem, vmem),

time: 44.4 us -> 39.7 us (0.89)
  the two profiles are of different devices: /device:TPU:6 before, /device:TPU:28 now
where the time goes in v1:
time: 39.7 us; the launch traced here: 39.5 us
  Pallas kernels  36.8 us (93%)
  local copies, waits for them, and re-layouts  1.45 us (4%)
  between operations  1.29 us (3%)
    pallas_call x1, Pallas kernels, fast_body(): pl.pallas_call(functools.partial(fused_kernel, halo, back), out_shape=(pl...  36.8 us
    unnamed x2, local copies, waits for them, and re-layouts  1.45 us

profile of v1, /device:TPU:28, one launch (start us, length us, event | category | flops | bytes accessed | tf_op | source)
XLA Modules:
  0.0 39.5 jit_solution(10994345577858230250)
XLA Ops:
  1.3 36.8 %shard_map.86 = (bf16[256,1024]{1,0:T(8,128)(2,1)S(1)}, bf16[256,256]{1,0:T(8,128)(2,1)S(1)}) custom-call(s32[1]{0:T(128)S(6)} %copy.13.window_ref, bf16[256,2048]{1,0:T(8,128)(2,1)} %hid_hbm.1, bf16[2048,128]{1,0:T(8,128)(2,1)} %w_hbm.1, bf16[256,1024]{1,0:T(8,128)(2,1)} %q_hbm.1, bf16[256]{0:T(256)(128)(2,1)} %bias_hbm.1, ...), custom_call_target="tpu_custom_call" | custom-call | tf_op jit(solution)/shard_map/pallas_call | solution.py:452
  38.1 0.8 %copy.11 = bf16[256,1024]{1,0:T(8,128)(2,1)} copy(bf16[256,1024]{1,0:T(8,128)(2,1)S(1)} %get-tuple-element.2) | data formatting | bytes 1048576
  38.9 0.7 %copy.12 = bf16[256,256]{1,0:T(8,128)(2,1)} copy(bf16[256,256]{1,0:T(8,128)(2,1)S(1)} %get-tuple-element.3) | data formatting | bytes 262144

commit v2 on v1

--- a/solution.py
+++ b/solution.py
@@ -118,10 +118,11 @@
 
 
 def fused_kernel(
-    halo, back, window_ref, hid_hbm, w_hbm, q_hbm, bias_hbm, freq_hbm, seg_hbm, out_ref, cache_ref,
+    halo, back, window_ref, hid_hbm, w_hbm, q_hbm, bias_hbm, freq_hbm, seg_hbm,
+    probs, totals, near, cache_ref,
     kv_ref, segs_ref, hbuf, wbuf, part_out, part_in, own, cosb, sinb,
-    q_ref, bias_ref, freq_ref, seg_line, seg_ref, mask, probs, totals,
-    local_sem, hid_sem, gate, wsend, wrecv, psend, precv, ksend, krecv, fsend, frecv, ssend, srecv,
+    q_ref, bias_ref, freq_ref, seg_line, seg_ref, mask, begun,
+    local_sem, hid_sem, gate, clear, wsend, wrecv, relay_recv, psend, precv, ksend, krecv, fsend, frecv, ssend, srecv,
 ):
     c = lax.axis_index("ctx")
     t = lax.axis_index("tp")
@@ -166,16 +167,27 @@
         other_y = 1 - pair // 2 if d // 2 else pair // 2
         return other_y * 2 + other_x
 
-    def w_copy(src, dst, q, sem, to):
+    def w_copy(src, dst, q, to):
         return pltpu.make_async_remote_copy(
             src_ref=wbuf.at[src, q], dst_ref=wbuf.at[dst, q],
-            send_sem=wsend.at[sem], recv_sem=wrecv.at[dst, q],
+            send_sem=wsend, recv_sem=wrecv.at[dst - 1, q],
             device_id=(2 * neighbour(to) + core, t), device_id_type=MESH,
         )
 
-    x_first, x_second = w_copy(0, 1, 0, 0, 1), w_copy(0, 1, 1, 1, 1)
-    y_first, y_second = w_copy(0, 2, 1, 2, 2), w_copy(0, 2, 0, 3, 2)
-    relay_y, relay_x = w_copy(1, 3, 0, 4, 2), w_copy(2, 3, 1, 5, 1)
+    x_first, x_second = w_copy(0, 1, 0, 1), w_copy(0, 1, 1, 1)
+    y_first, y_second = w_copy(0, 2, 1, 2), w_copy(0, 2, 0, 2)
+    quarter = half // 2
+
+    def relay_copy(src, q, part, to):
+        rows = pl.ds(part * quarter, quarter)
+        return pltpu.make_async_remote_copy(
+            src_ref=wbuf.at[src, q, rows], dst_ref=wbuf.at[3, q, rows],
+            send_sem=wsend, recv_sem=relay_recv.at[q, part],
+            device_id=(2 * neighbour(to) + core, t), device_id_type=MESH,
+        )
+
+    relay_y = [relay_copy(1, 0, part, 2) for part in range(2)]
+    relay_x = [relay_copy(2, 1, part, 1) for part in range(2)]
 
     def send_weights():
         x_first.start()
@@ -225,31 +237,39 @@
                 segs_ref[:, rows] = jnp.full((segs_ref.shape[0], span), -1, jnp.int32)
                 kv_ref[:, rows, :] = jnp.zeros((2, span, head), jnp.bfloat16)
 
-    def multiply(d):
-        acc = jnp.dot(hbuf[:, :half], wbuf[d, 0], preferred_element_type=jnp.float32)
-        return acc + jnp.dot(hbuf[:, half:], wbuf[d, 1], preferred_element_type=jnp.float32)
-
-    def part_copy(d):
+    low, high = slice(0, toks), slice(toks, span)
+    token_halves = (low, high)
+
+    def product(rows, features, weights):
+        return jnp.dot(hbuf[rows, features], weights, preferred_element_type=jnp.float32)
+
+    def part_copy(d, r):
         return pltpu.make_async_remote_copy(
-            src_ref=part_out.at[d], dst_ref=part_in.at[t],
-            send_sem=psend.at[d], recv_sem=precv.at[t],
+            src_ref=part_out.at[d, token_halves[r]], dst_ref=part_in.at[t, token_halves[r]],
+            send_sem=psend, recv_sem=precv.at[t, r],
             device_id=(c, neighbour(d)), device_id_type=MESH,
         )
 
-    def hand_over(d):
-        acc = multiply(d)
-        part_out[d] = acc.astype(part_out.dtype)
+    def hand_over(d, r, acc):
+        rows = token_halves[r]
+        part_out[d, rows] = acc.astype(part_out.dtype)
 
         @pl.when(neighbour(d) == t)
         def _():
-            own[...] = acc
+            own[rows] = acc
 
         @pl.when(neighbour(d) != t)
         def _():
-            part_copy(d).start()
+            part_copy(d, r).start()
+
+    def whole(q):
+        return slice(q * half, (q + 1) * half)
 
     hid.wait()
-    hand_over(0)
+    every = slice(0, span)
+    local = product(every, whole(0), wbuf[0, 0]) + product(every, whole(1), wbuf[0, 1])
+    for r in range(2):
+        hand_over(0, r, local[token_halves[r]])
 
     @pl.when(core == 1)
     def _():
@@ -257,9 +277,11 @@
         send_weights()
 
     x_first.wait_recv()
-    relay_y.start()
+    for copy in relay_y:
+        copy.start()
     y_first.wait_recv()
-    relay_x.start()
+    for copy in relay_x:
+        copy.start()
 
     angle_rows = (lax.broadcasted_iota(jnp.int32, (span, head), 0) + pair * span).astype(jnp.float32)
     angles = angle_rows * freq_ref[0:1, :]
@@ -276,8 +298,20 @@
     def _():
         pl.semaphore_signal(gate, inc=1, device_id=(mate, t), device_id_type=MESH)
 
-    hand_over(1)
-    hand_over(2)
+    both = sum(
+        product(every, whole(q), jnp.concatenate([wbuf[1, q], wbuf[2, q]], axis=1)) for q in range(2)
+    )
+    for d in (1, 2):
+        for r in range(2):
+            hand_over(d, r, both[token_halves[r], (d - 1) * head : d * head])
+    pltpu.make_async_remote_copy(
+        src_ref=wbuf.at[pl.ds(0, 3)], dst_ref=wbuf.at[pl.ds(0, 3)],
+        send_sem=wsend, recv_sem=wrecv.at[0, 0], device_id=(mate, t), device_id_type=MESH,
+    ).wait_send()
+
+    @pl.when(core == 1)
+    def _():
+        pl.semaphore_signal(clear, inc=1, device_id=(mate, t), device_id_type=MESH)
 
     def seg_arrival(step, sub):
         at = pl.ds(pl.multiple_of((back - step) * span + sub * toks, toks), toks)
@@ -307,64 +341,83 @@
     )
     mask[...] = jnp.where(allowed, 0.0, -jnp.inf)
 
-    relay_y.wait_recv()
-    relay_x.wait_recv()
-    for copy in (x_first, x_second, y_first, y_second, relay_y, relay_x):
-        copy.wait_send()
-
-    hand_over(3)
-
-    def kv_copy(kind, src_step, dst_step, send, recv, to):
+    def far(rows, part):
+        return sum(
+            product(
+                rows, slice(q * half + part * quarter, q * half + (part + 1) * quarter),
+                wbuf[3, q, part * quarter : (part + 1) * quarter],
+            )
+            for q in range(2)
+        )
+
+    relay_y[0].wait_recv()
+    relay_x[0].wait_recv()
+    begun[...] = far(every, 0)
+    relay_y[1].wait_recv()
+    relay_x[1].wait_recv()
+    for r in range(2):
+        hand_over(3, r, begun[token_halves[r]] + far(token_halves[r], 1))
+
+    def rows_of(step, r):
+        return pl.ds((back - step) * span + r * toks, toks)
+
+    def kv_copy(kind, src_step, dst_step, r, send, recv, to):
         return pltpu.make_async_remote_copy(
-            src_ref=kv_ref.at[kind, pl.ds((back - src_step) * span, span)],
-            dst_ref=kv_ref.at[kind, pl.ds((back - dst_step) * span, span)],
-            send_sem=send, recv_sem=recv, device_id=(to, t), device_id_type=MESH,
-        )
-
-    def onward(step):
+            src_ref=kv_ref.at[kind, rows_of(src_step, r)],
+            dst_ref=kv_ref.at[kind, rows_of(dst_step, r)],
+            send_sem=send.at[dst_step], recv_sem=recv.at[dst_step, r],
+            device_id=(to, t), device_id_type=MESH,
+        )
+
+    def onward(step, r):
         to = jnp.minimum(2 * (pair + step) + core, n_ctx - 2 + core)
-        return kv_copy(core, 0, step, ksend.at[step], krecv.at[step], to)
-
-    def across(step):
-        return kv_copy(core, step, step, fsend.at[step], frecv.at[step], mate)
-
-    def crossed(step):
-        return kv_copy(1 - core, step, step, fsend.at[step], frecv.at[step], mate)
+        return kv_copy(core, 0, step, r, ksend, krecv, to)
+
+    def across(step, r):
+        return kv_copy(core, step, step, r, fsend, frecv, mate)
+
+    def crossed(step, r):
+        return kv_copy(1 - core, step, step, r, fsend, frecv, mate)
 
     def finish(rotated):
-        total = own[...] + bias_ref[...].reshape(1, 2 * head)[:, :head].astype(jnp.float32) if rotated else (
-            own[...] + bias_ref[...].reshape(1, 2 * head)[:, head:].astype(jnp.float32)
-        )
-        for step in range(1, n_tp):
-            source = (t + step) % n_tp
-            pltpu.make_async_remote_copy(
-                src_ref=part_out.at[0], dst_ref=part_in.at[source],
-                send_sem=psend.at[0], recv_sem=precv.at[source],
-                device_id=(c, source), device_id_type=MESH,
-            ).wait_recv()
-            total = total + part_in[source].astype(jnp.float32)
-        if rotated:
-            total = total * cosb[...] + pltpu.roll(total, head // 2, 1) * sinb[...]
-        kv_ref[0 if rotated else 1, back * span :, :] = total.astype(jnp.bfloat16)
-        across(0).start()
-        for step in range(1, back + 1):
-            @pl.when(pair + step < pairs)
-            def _():
-                onward(step).start()
+        bias = bias_ref[...].reshape(1, 2 * head).astype(jnp.float32)
+        bias = bias[:, :head] if rotated else bias[:, head:]
+        for r in range(2):
+            rows = token_halves[r]
+            total = own[rows] + bias
+            for step in range(1, n_tp):
+                source = (t + step) % n_tp
+                pltpu.make_async_remote_copy(
+                    src_ref=part_out.at[0, rows], dst_ref=part_in.at[source, rows],
+                    send_sem=psend, recv_sem=precv.at[source, r],
+                    device_id=(c, source), device_id_type=MESH,
+                ).wait_recv()
+                total = total + part_in[source, rows].astype(jnp.float32)
+            if rotated:
+                total = total * cosb[rows] + pltpu.roll(total, head // 2, 1) * sinb[rows]
+            kv_ref[0 if rotated else 1, rows_of(0, r), :] = total.astype(jnp.bfloat16)
+            across(0, r).start()
+            if rotated and r == 0:
+                pl.semaphore_wait(clear, 1)
+            for step in range(1, back + 1):
+                @pl.when(pair + step < pairs)
+                def _():
+                    onward(step, r).start()
 
     def pass_on():
-        for step in range(1, back + 1):
+        for r in range(2):
+            for step in range(1, back + 1):
+                @pl.when(pair >= step)
+                def _():
+                    onward(step, r).wait_recv()
+                    across(step, r).start()
+
+    def await_crossed():
+        for step in range(back + 1):
             @pl.when(pair >= step)
             def _():
-                onward(step).wait_recv()
-                across(step).start()
-
-    def await_crossed():
-        crossed(0).wait_recv()
-        for step in range(1, back + 1):
-            @pl.when(pair >= step)
-            def _():
-                crossed(step).wait_recv()
+                for r in range(2):
+                    crossed(step, r).wait_recv()
 
     def weigh(lower, upper):
         keys = kv_ref[0, pl.ds(start, width), :]
@@ -389,7 +442,9 @@
         lax.fori_loop(lower // 2, upper // 2, couple, 0)
 
     group = q_ref.shape[1] // head
-    early = group // 2
+    early = group // 4 * 2
+    behind = pair - (n_tp - 1 - t)
+    waits_long = (behind >= 1) & (behind <= back)
 
     @pl.when(core == 0)
     def _():
@@ -400,41 +455,66 @@
 
     @pl.when(core == 1)
     def _():
+        finish(False)
         await_crossed()
         weigh(0, early)
-        finish(False)
+
+        @pl.when(jnp.logical_not(waits_long))
+        def _():
+            pass_on()
+
         weigh(early, group)
-        pass_on()
-
-    values = kv_ref[1, pl.ds(start, width), :]
-
-    def mix(i, carry):
-        for h in (2 * i, 2 * i + 1):
-            lanes = pl.ds(pl.multiple_of(h * head, head), head)
-            mixed = jnp.dot(probs[h], values, preferred_element_type=jnp.float32)
-            out_ref[:, lanes] = (mixed / totals[h]).astype(out_ref.dtype)
-        return carry
-
-    lax.fori_loop(0, group // 2, mix, 0)
+
+        @pl.when(waits_long)
+        def _():
+            pass_on()
+
+    near[...] = kv_ref[1, pl.ds(start, width), :]
     cache_ref[:, :head] = kv_ref[0, here, :]
     cache_ref[:, head:] = kv_ref[1, here, :]
 
-    for d in range(n_tp):
-        @pl.when(neighbour(d) != t)
-        def _():
-            part_copy(d).wait_send()
+    pltpu.make_async_remote_copy(
+        src_ref=part_out.at[pl.ds(0, n_tp - 1)], dst_ref=part_in.at[pl.ds(0, n_tp - 1)],
+        send_sem=psend, recv_sem=precv.at[0, 0], device_id=(mate, t), device_id_type=MESH,
+    ).wait_send()
+
+    def sent(sem):
+        block = kv_ref.at[0, pl.ds(0, span)]
+        pltpu.make_async_remote_copy(
+            src_ref=block, dst_ref=block, send_sem=sem, recv_sem=krecv.at[0, 0],
+            device_id=(mate, t), device_id_type=MESH,
+        ).wait_send()
+
+    sent(fsend.at[0])
     seg_copy(0, 0).wait_send()
-    across(0).wait_send()
     for step in range(1, back + 1):
         @pl.when(pair + step < pairs)
         def _():
+            sent(ksend.at[step])
             seg_copy(step, 0).wait_send()
             seg_copy(step, 1).wait_send()
-            onward(step).wait_send()
 
         @pl.when(pair >= step)
         def _():
-            across(step).wait_send()
+            sent(fsend.at[step])
+
+
+def mix_kernel(probs, totals, near, cache_ref, out_hbm, cache_hbm, mixed, sems):
+    group, _, head = mixed.shape
+    cache_copy = pltpu.make_async_copy(cache_ref, cache_hbm, sems.at[group])
+    cache_copy.start()
+
+    def out_copy(h):
+        lanes = pl.ds(h * head, head)
+        return pltpu.make_async_copy(mixed.at[h], out_hbm.at[:, lanes], sems.at[h])
+
+    for h in range(group):
+        total = jnp.dot(probs[h], near[...], preferred_element_type=jnp.float32)
+        mixed[h] = (total / totals[h]).astype(mixed.dtype)
+        out_copy(h).start()
+    for h in range(group):
+        out_copy(h).wait()
+    cache_copy.wait()
 
 
 def fast_body(halo, back, hidden, queries, kv_weight, kv_bias, window, segment_ids):
@@ -447,16 +527,23 @@
     freqs = np.tile(np.concatenate([freqs, freqs])[None, :], (8, 1)).astype(np.float32)
     keys = (back + 1) * span
     vmem = pl.BlockSpec(memory_space=pltpu.VMEM)
-    hbm = pl.BlockSpec(memory_space=pl.ANY)
+    hbm = pl.BlockSpec(memory_space=pltpu.HBM)
     dma = pltpu.SemaphoreType.DMA
-    return pl.pallas_call(
+    width = halo + toks
+    operands = [
+        pltpu.with_memory_space_constraint(array, pltpu.HBM)
+        for array in (hidden, kv_weight, queries, kv_bias, jnp.asarray(freqs), segment_ids)
+    ]
+    made = pl.pallas_call(
         functools.partial(fused_kernel, halo, back),
         out_shape=(
-            pltpu.VMEM(queries.shape, jnp.bfloat16),
+            pltpu.VMEM((group, toks, width), jnp.bfloat16),
+            pltpu.VMEM((group, toks, 1), jnp.float32),
+            pltpu.VMEM((width, head), jnp.bfloat16),
             pltpu.VMEM((toks, 2 * head), jnp.bfloat16),
         ),
         in_specs=[pl.BlockSpec(memory_space=pltpu.SMEM), hbm, hbm, hbm, hbm, hbm, hbm],
-        out_specs=(vmem, vmem),
+        out_specs=(vmem,) * 4,
         scratch_shapes=[
             pltpu.VMEM((2, keys, head), jnp.bfloat16),
             pltpu.VMEM((8, keys), jnp.int32),
@@ -472,25 +559,40 @@
             pltpu.VMEM((8, head), jnp.float32),
             pltpu.VMEM((toks,), jnp.int32),
             pltpu.VMEM((8, toks), jnp.int32),
-            pltpu.VMEM((toks, halo + toks), jnp.float32),
-            pltpu.VMEM((group, toks, halo + toks), jnp.bfloat16),
-            pltpu.VMEM((group, toks, 1), jnp.float32),
+            pltpu.VMEM((toks, width), jnp.float32),
+            pltpu.VMEM((span, head), jnp.float32),
             dma((7,)),
             dma((2,)),
             pltpu.SemaphoreType.REGULAR,
-            dma((6,)),
+            pltpu.SemaphoreType.REGULAR,
+            dma,
+            dma((2, 2)),
+            dma((2, 2)),
+            dma,
             dma((n_tp, 2)),
-            dma((n_tp,)),
-            dma((n_tp,)),
             dma((back + 1,)),
+            dma((back + 1, 2)),
             dma((back + 1,)),
-            dma((back + 1,)),
-            dma((back + 1,)),
+            dma((back + 1, 2)),
             dma((2 * back + 2,)),
             dma((2 * back + 2,)),
         ],
-        compiler_params=pltpu.CompilerParams(collective_id=0, has_side_effects=True),
-    )(window, hidden, kv_weight, queries, kv_bias, jnp.asarray(freqs), segment_ids)
+        compiler_params=pltpu.CompilerParams(
+            collective_id=0, has_side_effects=True, vmem_limit_bytes=32 << 20
+        ),
+    )(window, *operands)
+    made = [pltpu.with_memory_space_constraint(array, pltpu.VMEM) for array in made]
+    return pl.pallas_call(
+        mix_kernel,
+        out_shape=(
+            jax.ShapeDtypeStruct(queries.shape, jnp.bfloat16),
+            jax.ShapeDtypeStruct((toks, 2 * head), jnp.bfloat16),
+        ),
+        in_specs=[vmem] * 4,
+        out_specs=(hbm, hbm),
+        scratch_shapes=[pltpu.VMEM((group, toks, head), jnp.bfloat16), dma((group + 1,))],
+        compiler_params=pltpu.CompilerParams(vmem_limit_bytes=32 << 20),
+    )(*made)
 
 
 def solution(mesh):

time: 39.7 us -> 37.9 us (0.955)
  the two profiles are of different devices: /device:TPU:28 before, /device:TPU:5 now
where the time goes in v2:
time: 37.9 us; the launch traced here: 37.3 us
  Pallas kernels  36.1 us (95%)
  between operations  1.29 us (3%)
    pallas_call x1, Pallas kernels, fast_body(): pl.pallas_call(functools.partial(fused_kernel, halo, back), out_shape=(pl...  33.8 us
    pallas_call x1, Pallas kernels, fast_body(): pl.pallas_call(mix_kernel, out_shape=(jax.ShapeDtypeStruct(queries.shape,...  2.23 us

profile of v2, /device:TPU:5, one launch (start us, length us, event | category | flops | bytes accessed | tf_op | source)
XLA Modules:
  0.0 37.3 jit_solution(17566106015530445816)
XLA Ops:
  1.3 33.8 %shard_map.86 = (bf16[8,256,1280]{2,1,0:T(8,128)(2,1)S(1)}, f32[8,256,1]{2,1,0:T(8,128)S(1)}, bf16[1280,128]{1,0:T(8,128)(2,1)S(1)}, bf16[256,256]{1,0:T(8,128)(2,1)S(1)}) custom-call(s32[1]{0:T(128)S(6)} %copy.9.window_ref, bf16[256,2048]{1,0:T(8,128)(2,1)} %hid_hbm.1, bf16[2048,128]{1,0:T(8,128)(2,1)} %w_hbm.1, bf16[256,1024]{1,0:T(8,128)(2,1)} %q_hbm.1, ...), custom_call_target="tpu_custom_call" | custom-call | tf_op jit(solution)/shard_map/pallas_call | solution.py:537
  35.1 2.2 %shard_map.87 = (bf16[256,1024]{1,0:T(8,128)(2,1)}, bf16[256,256]{1,0:T(8,128)(2,1)}) custom-call(bf16[8,256,1280]{2,1,0:T(8,128)(2,1)S(1)} %get-tuple-element.6.probs, f32[8,256,1]{2,1,0:T(8,128)S(1)} %get-tuple-element.7.totals, bf16[1280,128]{1,0:T(8,128)(2,1)S(1)} %get-tuple-element.8.near, bf16[256,256]{1,0:T(8,128)(2,1)S(1)} %get-tuple-element.9.cache_ref), custom_call_target="tpu_custom_call" | custom-call | tf_op jit(solution)/shard_map/pallas_call | solution.py:585

commit v3 on v2

--- a/solution.py
+++ b/solution.py
@@ -11,6 +11,7 @@
 WINDOW = 4096
 MESH = pl.DeviceIdType.MESH
 LOG2E = 1.4426950408889634
+LOWEST = -1e30
 
 
 rope_base = 1000000.0
@@ -119,7 +120,7 @@
 
 def fused_kernel(
     halo, back, window_ref, hid_hbm, w_hbm, q_hbm, bias_hbm, freq_hbm, seg_hbm,
-    probs, totals, near, cache_ref,
+    probs, tops, totals, near, cache_ref,
     kv_ref, segs_ref, hbuf, wbuf, part_out, part_in, own, cosb, sinb,
     q_ref, bias_ref, freq_ref, seg_line, seg_ref, mask, begun,
     local_sem, hid_sem, gate, clear, wsend, wrecv, relay_recv, psend, precv, ksend, krecv, fsend, frecv, ssend, srecv,
@@ -412,15 +413,15 @@
                     onward(step, r).wait_recv()
                     across(step, r).start()
 
-    def await_crossed():
-        for step in range(back + 1):
+    def await_crossed(steps):
+        for step in steps:
             @pl.when(pair >= step)
             def _():
                 for r in range(2):
                     crossed(step, r).wait_recv()
 
-    def weigh(lower, upper):
-        keys = kv_ref[0, pl.ds(start, width), :]
+    def weigh(part, first, last, lower, upper):
+        keys = kv_ref[0, pl.ds(pl.multiple_of(start + first, toks), last - first), :]
         scale = head ** (-0.5) * LOG2E
 
         def one(h):
@@ -428,11 +429,12 @@
             scores = lax.dot_general(
                 q_ref[:, lanes], keys, (((1,), (1,)), ((), ())), preferred_element_type=jnp.float32
             )
-            scores = scores + mask[...]
-            top = jnp.max(scores, axis=1, keepdims=True)
+            scores = scores + mask[:, first:last]
+            top = jnp.maximum(jnp.max(scores, axis=1, keepdims=True), LOWEST)
             weights = jnp.exp2((scores - top) * scale)
-            totals[h] = jnp.sum(weights, axis=1, keepdims=True)
-            probs[h] = weights.astype(jnp.bfloat16)
+            tops[part, h] = top
+            totals[part, h] = jnp.sum(weights, axis=1, keepdims=True)
+            probs[h, :, first:last] = weights.astype(jnp.bfloat16)
 
         def couple(i, carry):
             one(2 * i)
@@ -449,21 +451,25 @@
     @pl.when(core == 0)
     def _():
         finish(True)
+        weigh(0, halo, width, 0, group)
         pass_on()
-        weigh(0, group)
-        await_crossed()
+        weigh(1, 0, halo, 0, group)
+        await_crossed(range(back + 1))
 
     @pl.when(core == 1)
     def _():
+        split = halo - toks
+        await_crossed([0])
+        weigh(0, split, width, 0, group)
         finish(False)
-        await_crossed()
-        weigh(0, early)
+        await_crossed(range(1, back + 1))
+        weigh(1, 0, split, 0, early)
 
         @pl.when(jnp.logical_not(waits_long))
         def _():
             pass_on()
 
-        weigh(early, group)
+        weigh(1, 0, split, early, group)
 
         @pl.when(waits_long)
         def _():
@@ -499,8 +505,10 @@
             sent(fsend.at[step])
 
 
-def mix_kernel(probs, totals, near, cache_ref, out_hbm, cache_hbm, mixed, sems):
-    group, _, head = mixed.shape
+def mix_kernel(probs, tops, totals, near, cache_ref, out_hbm, cache_hbm, mixed, sems):
+    group, toks, head = mixed.shape
+    width = near.shape[0]
+    scale = head ** (-0.5) * LOG2E
     cache_copy = pltpu.make_async_copy(cache_ref, cache_hbm, sems.at[group])
     cache_copy.start()
 
@@ -508,10 +516,26 @@
         lanes = pl.ds(h * head, head)
         return pltpu.make_async_copy(mixed.at[h], out_hbm.at[:, lanes], sems.at[h])
 
-    for h in range(group):
-        total = jnp.dot(probs[h], near[...], preferred_element_type=jnp.float32)
-        mixed[h] = (total / totals[h]).astype(mixed.dtype)
-        out_copy(h).start()
+    def mix(split):
+        for h in range(group):
+            highest = jnp.maximum(tops[0, h], tops[1, h])
+            lift = [jnp.exp2((tops[part, h] - highest) * scale) for part in range(2)]
+            total = lift[0] * totals[0, h] + lift[1] * totals[1, h]
+            own = jnp.dot(probs[h, :, split:], near[split:], preferred_element_type=jnp.float32)
+            far = jnp.dot(probs[h, :, :split], near[:split], preferred_element_type=jnp.float32)
+            mixed[h] = (own * (lift[0] / total) + far * (lift[1] / total)).astype(mixed.dtype)
+            out_copy(h).start()
+
+    core = lax.axis_index("ctx") % 2
+
+    @pl.when(core == 0)
+    def _():
+        mix(width - toks)
+
+    @pl.when(core == 1)
+    def _():
+        mix(width - 2 * toks)
+
     for h in range(group):
         out_copy(h).wait()
     cache_copy.wait()
@@ -538,12 +562,13 @@
         functools.partial(fused_kernel, halo, back),
         out_shape=(
             pltpu.VMEM((group, toks, width), jnp.bfloat16),
-            pltpu.VMEM((group, toks, 1), jnp.float32),
+            pltpu.VMEM((2, group, toks, 1), jnp.float32),
+            pltpu.VMEM((2, group, toks, 1), jnp.float32),
             pltpu.VMEM((width, head), jnp.bfloat16),
             pltpu.VMEM((toks, 2 * head), jnp.bfloat16),
         ),
         in_specs=[pl.BlockSpec(memory_space=pltpu.SMEM), hbm, hbm, hbm, hbm, hbm, hbm],
-        out_specs=(vmem,) * 4,
+        out_specs=(vmem,) * 5,
         scratch_shapes=[
             pltpu.VMEM((2, keys, head), jnp.bfloat16),
             pltpu.VMEM((8, keys), jnp.int32),
@@ -588,7 +613,7 @@
             jax.ShapeDtypeStruct(queries.shape, jnp.bfloat16),
             jax.ShapeDtypeStruct((toks, 2 * head), jnp.bfloat16),
         ),
-        in_specs=[vmem] * 4,
+        in_specs=[vmem] * 5,
         out_specs=(hbm, hbm),
         scratch_shapes=[pltpu.VMEM((group, toks, head), jnp.bfloat16), dma((group + 1,))],
         compiler_params=pltpu.CompilerParams(vmem_limit_bytes=32 << 20),

time: 37.9 us -> 36.3 us (0.958); the launches traced: 37.3 us -> 36.1 us
  Pallas kernels: 36.1 us -> 34.8 us
    pallas_call x1, Pallas kernels: 33.8 us -> 32.5 us  [fast_body(): pl.pallas_call(functools.partial(fused_kernel, halo, back), out_shape=(pl...]
where the time goes in v3:
time: 36.3 us; the launch traced here: 36.1 us
  Pallas kernels  34.8 us (96%)
  between operations  1.29 us (4%)
    pallas_call x1, Pallas kernels, fast_body(): pl.pallas_call(functools.partial(fused_kernel, halo, back), out_shape=(pl...  32.5 us
    pallas_call x1, Pallas kernels, fast_body(): pl.pallas_call(mix_kernel, out_shape=(jax.ShapeDtypeStruct(queries.shape,...  2.3 us

profile of v3, /device:TPU:5, one launch (start us, length us, event | category | flops | bytes accessed | tf_op | source)
XLA Modules:
  0.0 36.1 jit_solution(8866404336537055977)
XLA Ops:
  1.3 32.5 %shard_map.86 = (bf16[8,256,1280]{2,1,0:T(8,128)(2,1)S(1)}, f32[2,8,256,1]{3,2,1,0:T(8,128)S(1)}, f32[2,8,256,1]{3,2,1,0:T(8,128)S(1)}, bf16[1280,128]{1,0:T(8,128)(2,1)S(1)}, bf16[256,256]{1,0:T(8,128)(2,1)S(1)}) custom-call(s32[1]{0:T(128)S(6)} %copy.9.window_ref, bf16[256,2048]{1,0:T(8,128)(2,1)} %hid_hbm.1, bf16[2048,128]{1,0:T(8,128)(2,1)} %w_hbm.1, ...), custom_call_target="tpu_custom_call" | custom-call | tf_op jit(solution)/shard_map/pallas_call | solution.py:561
  33.8 2.3 %shard_map.87 = (bf16[256,1024]{1,0:T(8,128)(2,1)}, bf16[256,256]{1,0:T(8,128)(2,1)}) custom-call(bf16[8,256,1280]{2,1,0:T(8,128)(2,1)S(1)} %get-tuple-element.7.probs, f32[2,8,256,1]{3,2,1,0:T(8,128)S(1)} %get-tuple-element.8.tops, f32[2,8,256,1]{3,2,1,0:T(8,128)S(1)} %get-tuple-element.9.totals, bf16[1280,128]{1,0:T(8,128)(2,1)S(1)} %get-tuple-element.10.near, ...), custom_call_target="tpu_custom_call" | custom-call | tf_op jit(solution)/shard_map/pallas_call | solution.py:610

commit v4 on v3

--- a/solution.py
+++ b/solution.py
@@ -120,7 +120,7 @@
 
 def fused_kernel(
     halo, back, window_ref, hid_hbm, w_hbm, q_hbm, bias_hbm, freq_hbm, seg_hbm,
-    probs, tops, totals, near, cache_ref,
+    probs, tops, base, near, cache_ref,
     kv_ref, segs_ref, hbuf, wbuf, part_out, part_in, own, cosb, sinb,
     q_ref, bias_ref, freq_ref, seg_line, seg_ref, mask, begun,
     local_sem, hid_sem, gate, clear, wsend, wrecv, relay_recv, psend, precv, ksend, krecv, fsend, frecv, ssend, srecv,
@@ -183,7 +183,7 @@
         rows = pl.ds(part * quarter, quarter)
         return pltpu.make_async_remote_copy(
             src_ref=wbuf.at[src, q, rows], dst_ref=wbuf.at[3, q, rows],
-            send_sem=wsend, recv_sem=relay_recv.at[q, part],
+            send_sem=wsend, recv_sem=relay_recv.at[part],
             device_id=(2 * neighbour(to) + core, t), device_id_type=MESH,
         )
 
@@ -217,7 +217,7 @@
         at = pl.ds(pl.multiple_of((back - step) * span + core * toks, toks), toks)
         return pltpu.make_async_remote_copy(
             src_ref=seg_ref, dst_ref=segs_ref.at[:, at],
-            send_sem=ssend.at[2 * step + sub], recv_sem=srecv.at[2 * step + core],
+            send_sem=ssend.at[step], recv_sem=srecv.at[step],
             device_id=(jnp.minimum(2 * (pair + step) + sub, n_ctx - 1) if step else mate, t),
             device_id_type=MESH,
         )
@@ -247,7 +247,7 @@
     def part_copy(d, r):
         return pltpu.make_async_remote_copy(
             src_ref=part_out.at[d, token_halves[r]], dst_ref=part_in.at[t, token_halves[r]],
-            send_sem=psend, recv_sem=precv.at[t, r],
+            send_sem=psend, recv_sem=precv.at[(t - neighbour(d) + n_tp - 1) % n_tp, r],
             device_id=(c, neighbour(d)), device_id_type=MESH,
         )
 
@@ -292,19 +292,19 @@
     cosb[...] = jnp.where(is_key, jnp.cos(angles), 1.0)
     sinb[...] = jnp.where(is_key, jnp.where(left, -sine, sine), 0.0)
 
+    for d in (1, 2):
+        begun[d - 1] = product(every, whole(d - 1), wbuf[d, d - 1])
+    y_second.wait_recv()
     x_second.wait_recv()
-    y_second.wait_recv()
 
     @pl.when(core == 0)
     def _():
         pl.semaphore_signal(gate, inc=1, device_id=(mate, t), device_id_type=MESH)
 
-    both = sum(
-        product(every, whole(q), jnp.concatenate([wbuf[1, q], wbuf[2, q]], axis=1)) for q in range(2)
-    )
-    for d in (1, 2):
+    for d in (2, 1):
+        full = begun[d - 1] + product(every, whole(2 - d), wbuf[d, 2 - d])
         for r in range(2):
-            hand_over(d, r, both[token_halves[r], (d - 1) * head : d * head])
+            hand_over(d, r, full[token_halves[r]])
     pltpu.make_async_remote_copy(
         src_ref=wbuf.at[pl.ds(0, 3)], dst_ref=wbuf.at[pl.ds(0, 3)],
         send_sem=wsend, recv_sem=wrecv.at[0, 0], device_id=(mate, t), device_id_type=MESH,
@@ -314,20 +314,18 @@
     def _():
         pl.semaphore_signal(clear, inc=1, device_id=(mate, t), device_id_type=MESH)
 
-    def seg_arrival(step, sub):
-        at = pl.ds(pl.multiple_of((back - step) * span + sub * toks, toks), toks)
+    def seg_block(step, count):
+        block = segs_ref.at[:, pl.ds((back - step) * span, count * toks)]
         return pltpu.make_async_remote_copy(
-            src_ref=seg_ref, dst_ref=segs_ref.at[:, at],
-            send_sem=ssend.at[0], recv_sem=srecv.at[2 * step + sub],
+            src_ref=block, dst_ref=block, send_sem=ssend.at[step], recv_sem=srecv.at[step],
             device_id=(mate, t), device_id_type=MESH,
         )
 
-    seg_arrival(0, 1 - core).wait_recv()
+    seg_block(0, 1).wait_recv()
     for step in range(1, back + 1):
         @pl.when(pair >= step)
         def _():
-            seg_arrival(step, 0).wait_recv()
-            seg_arrival(step, 1).wait_recv()
+            seg_block(step, 2).wait_recv()
 
     width = halo + toks
     start = pl.multiple_of((core + 2 * back) * toks - halo, toks)
@@ -351,13 +349,18 @@
             for q in range(2)
         )
 
-    relay_y[0].wait_recv()
-    relay_x[0].wait_recv()
-    begun[...] = far(every, 0)
-    relay_y[1].wait_recv()
-    relay_x[1].wait_recv()
+    def relayed(part):
+        pltpu.make_async_remote_copy(
+            src_ref=wbuf.at[3, 0], dst_ref=wbuf.at[3, 0],
+            send_sem=wsend, recv_sem=relay_recv.at[part],
+            device_id=(mate, t), device_id_type=MESH,
+        ).wait_recv()
+
+    relayed(0)
+    begun[0] = far(every, 0)
+    relayed(1)
     for r in range(2):
-        hand_over(3, r, begun[token_halves[r]] + far(token_halves[r], 1))
+        hand_over(3, r, begun[0, token_halves[r]] + far(token_halves[r], 1))
 
     def rows_of(step, r):
         return pl.ds((back - step) * span + r * toks, toks)
@@ -366,19 +369,23 @@
         return pltpu.make_async_remote_copy(
             src_ref=kv_ref.at[kind, rows_of(src_step, r)],
             dst_ref=kv_ref.at[kind, rows_of(dst_step, r)],
-            send_sem=send.at[dst_step], recv_sem=recv.at[dst_step, r],
+            send_sem=send, recv_sem=recv,
             device_id=(to, t), device_id_type=MESH,
         )
 
     def onward(step, r):
         to = jnp.minimum(2 * (pair + step) + core, n_ctx - 2 + core)
-        return kv_copy(core, 0, step, r, ksend, krecv, to)
+        return kv_copy(core, 0, step, r, ksend.at[step - 1], krecv.at[step - 1, r], to)
 
     def across(step, r):
-        return kv_copy(core, step, step, r, fsend, frecv, mate)
-
-    def crossed(step, r):
-        return kv_copy(1 - core, step, step, r, fsend, frecv, mate)
+        return kv_copy(core, step, step, r, fsend.at[step], frecv.at[step], mate)
+
+    def crossed(step):
+        block = kv_ref.at[1 - core, pl.ds((back - step) * span, span)]
+        return pltpu.make_async_remote_copy(
+            src_ref=block, dst_ref=block, send_sem=fsend.at[step], recv_sem=frecv.at[step],
+            device_id=(mate, t), device_id_type=MESH,
+        )
 
     def finish(rotated):
         bias = bias_ref[...].reshape(1, 2 * head).astype(jnp.float32)
@@ -390,7 +397,7 @@
                 source = (t + step) % n_tp
                 pltpu.make_async_remote_copy(
                     src_ref=part_out.at[0, rows], dst_ref=part_in.at[source, rows],
-                    send_sem=psend, recv_sem=precv.at[source, r],
+                    send_sem=psend, recv_sem=precv.at[step - 1, r],
                     device_id=(c, source), device_id_type=MESH,
                 ).wait_recv()
                 total = total + part_in[source, rows].astype(jnp.float32)
@@ -417,8 +424,7 @@
         for step in steps:
             @pl.when(pair >= step)
             def _():
-                for r in range(2):
-                    crossed(step, r).wait_recv()
+                crossed(step).wait_recv()
 
     def weigh(part, first, last, lower, upper):
         keys = kv_ref[0, pl.ds(pl.multiple_of(start + first, toks), last - first), :]
@@ -433,7 +439,6 @@
             top = jnp.maximum(jnp.max(scores, axis=1, keepdims=True), LOWEST)
             weights = jnp.exp2((scores - top) * scale)
             tops[part, h] = top
-            totals[part, h] = jnp.sum(weights, axis=1, keepdims=True)
             probs[h, :, first:last] = weights.astype(jnp.bfloat16)
 
         def couple(i, carry):
@@ -443,8 +448,24 @@
 
         lax.fori_loop(lower // 2, upper // 2, couple, 0)
 
+    def mix_own(first):
+        cache_ref[:, :head] = kv_ref[0, here, :]
+        cache_ref[:, head:] = kv_ref[1, here, :]
+        rows = pl.ds(pl.multiple_of(start + first, toks), width - first)
+        values = jnp.concatenate(
+            [kv_ref[1, rows, :], jnp.ones((width - first, head), jnp.bfloat16)], axis=1
+        )
+
+        def couple(i, carry):
+            for h in (2 * i, 2 * i + 1):
+                base[h] = jnp.dot(probs[h, :, first:], values, preferred_element_type=jnp.float32)
+            return carry
+
+        lax.fori_loop(0, group // 2, couple, 0)
+
     group = q_ref.shape[1] // head
     early = group // 4 * 2
+    most = group * 3 // 8 * 2
     behind = pair - (n_tp - 1 - t)
     waits_long = (behind >= 1) & (behind <= back)
 
@@ -454,30 +475,44 @@
         weigh(0, halo, width, 0, group)
         pass_on()
         weigh(1, 0, halo, 0, group)
-        await_crossed(range(back + 1))
+        await_crossed([0])
+        mix_own(halo)
+        await_crossed(range(1, back + 1))
 
     @pl.when(core == 1)
     def _():
         split = halo - toks
         await_crossed([0])
         weigh(0, split, width, 0, group)
-        finish(False)
-        await_crossed(range(1, back + 1))
-        weigh(1, 0, split, 0, early)
-
-        @pl.when(jnp.logical_not(waits_long))
+        is_last = (neighbour(n_tp - 1) == t) & (pair != back)
+
+        @pl.when(is_last)
         def _():
+            await_crossed(range(1, back + 1))
+            weigh(1, 0, split, 0, early)
+            finish(False)
+            weigh(1, 0, split, early, group)
             pass_on()
-
-        weigh(1, 0, split, early, group)
-
-        @pl.when(waits_long)
+            mix_own(split)
+
+        @pl.when(jnp.logical_not(is_last))
         def _():
-            pass_on()
-
-    near[...] = kv_ref[1, pl.ds(start, width), :]
-    cache_ref[:, :head] = kv_ref[0, here, :]
-    cache_ref[:, head:] = kv_ref[1, here, :]
+            finish(False)
+            mix_own(split)
+            await_crossed(range(1, back + 1))
+            weigh(1, 0, split, 0, most)
+
+            @pl.when(jnp.logical_not(waits_long))
+            def _():
+                pass_on()
+
+            weigh(1, 0, split, most, group)
+
+            @pl.when(waits_long)
+            def _():
+                pass_on()
+
+    near[...] = kv_ref[1, pl.ds(start, halo), :]
 
     pltpu.make_async_remote_copy(
         src_ref=part_out.at[pl.ds(0, n_tp - 1)], dst_ref=part_in.at[pl.ds(0, n_tp - 1)],
@@ -492,22 +527,21 @@
         ).wait_send()
 
     sent(fsend.at[0])
-    seg_copy(0, 0).wait_send()
+    seg_block(0, 1).wait_send()
     for step in range(1, back + 1):
         @pl.when(pair + step < pairs)
         def _():
-            sent(ksend.at[step])
-            seg_copy(step, 0).wait_send()
-            seg_copy(step, 1).wait_send()
+            sent(ksend.at[step - 1])
+            seg_block(step, 2).wait_send()
 
         @pl.when(pair >= step)
         def _():
             sent(fsend.at[step])
 
 
-def mix_kernel(probs, tops, totals, near, cache_ref, out_hbm, cache_hbm, mixed, sems):
+def mix_kernel(probs, tops, base, near, cache_ref, out_hbm, cache_hbm, mixed, sems):
     group, toks, head = mixed.shape
-    width = near.shape[0]
+    width = near.shape[0] + toks
     scale = head ** (-0.5) * LOG2E
     cache_copy = pltpu.make_async_copy(cache_ref, cache_hbm, sems.at[group])
     cache_copy.start()
@@ -517,13 +551,13 @@
         return pltpu.make_async_copy(mixed.at[h], out_hbm.at[:, lanes], sems.at[h])
 
     def mix(split):
+        values = jnp.concatenate([near[:split], jnp.ones((split, head), near.dtype)], axis=1)
         for h in range(group):
+            far = jnp.dot(probs[h, :, :split], values, preferred_element_type=jnp.float32)
             highest = jnp.maximum(tops[0, h], tops[1, h])
             lift = [jnp.exp2((tops[part, h] - highest) * scale) for part in range(2)]
-            total = lift[0] * totals[0, h] + lift[1] * totals[1, h]
-            own = jnp.dot(probs[h, :, split:], near[split:], preferred_element_type=jnp.float32)
-            far = jnp.dot(probs[h, :, :split], near[:split], preferred_element_type=jnp.float32)
-            mixed[h] = (own * (lift[0] / total) + far * (lift[1] / total)).astype(mixed.dtype)
+            joint = base[h] * lift[0] + far * lift[1]
+            mixed[h] = (joint[:, :head] / joint[:, head:]).astype(mixed.dtype)
             out_copy(h).start()
 
     core = lax.axis_index("ctx") % 2
@@ -563,8 +597,8 @@
         out_shape=(
             pltpu.VMEM((group, toks, width), jnp.bfloat16),
             pltpu.VMEM((2, group, toks, 1), jnp.float32),
-            pltpu.VMEM((2, group, toks, 1), jnp.float32),
-            pltpu.VMEM((width, head), jnp.bfloat16),
+            pltpu.VMEM((group, toks, 2 * head), jnp.float32),
+            pltpu.VMEM((halo, head), jnp.bfloat16),
             pltpu.VMEM((toks, 2 * head), jnp.bfloat16),
         ),
         in_specs=[pl.BlockSpec(memory_space=pltpu.SMEM), hbm, hbm, hbm, hbm, hbm, hbm],
@@ -585,22 +619,22 @@
             pltpu.VMEM((toks,), jnp.int32),
             pltpu.VMEM((8, toks), jnp.int32),
             pltpu.VMEM((toks, width), jnp.float32),
-            pltpu.VMEM((span, head), jnp.float32),
+            pltpu.VMEM((2, span, head), jnp.float32),
             dma((7,)),
             dma((2,)),
             pltpu.SemaphoreType.REGULAR,
             pltpu.SemaphoreType.REGULAR,
             dma,
             dma((2, 2)),
-            dma((2, 2)),
+            dma((2,)),
             dma,
-            dma((n_tp, 2)),
+            dma((n_tp - 1, 2)),
+            dma((back,)),
+            dma((back, 2)),
             dma((back + 1,)),
-            dma((back + 1, 2)),
             dma((back + 1,)),
-            dma((back + 1, 2)),
-            dma((2 * back + 2,)),
-            dma((2 * back + 2,)),
+            dma((back + 1,)),
+            dma((back + 1,)),
         ],
         compiler_params=pltpu.CompilerParams(
             collective_id=0, has_side_effects=True, vmem_limit_bytes=32 << 20

time: 36.3 us -> 35.2 us (0.970)
  Pallas kernels: 34.8 us -> 33.6 us
    pallas_call x1, Pallas kernels: 32.5 us -> 31.8 us  [fast_body(): pl.pallas_call(functools.partial(fused_kernel, halo, back), out_shape=(pl...]
    pallas_call x1, Pallas kernels: 2.3 us -> 1.84 us  [fast_body(): pl.pallas_call(mix_kernel, out_shape=(jax.ShapeDtypeStruct(queries.shape,...]
where the time goes in v4:
time: 35.2 us; the launch traced here: 34.9 us
  Pallas kernels  33.6 us (95%)
  between operations  1.29 us (4%)
    pallas_call x1, Pallas kernels, fast_body(): pl.pallas_call(functools.partial(fused_kernel, halo, back), out_shape=(pl...  31.8 us
    pallas_call x1, Pallas kernels, fast_body(): pl.pallas_call(mix_kernel, out_shape=(jax.ShapeDtypeStruct(queries.shape,...  1.84 us

profile of v4, /device:TPU:5, one launch (start us, length us, event | category | flops | bytes accessed | tf_op | source)
XLA Modules:
  0.0 34.9 jit_solution(1923464831262390938)
XLA Ops:
  1.3 31.8 %shard_map.86 = (bf16[8,256,1280]{2,1,0:T(8,128)(2,1)S(1)}, f32[2,8,256,1]{3,2,1,0:T(8,128)S(1)}, f32[8,256,256]{2,1,0:T(8,128)S(1)}, bf16[1024,128]{1,0:T(8,128)(2,1)S(1)}, bf16[256,256]{1,0:T(8,128)(2,1)S(1)}) custom-call(s32[1]{0:T(128)S(6)} %copy.9.window_ref, bf16[256,2048]{1,0:T(8,128)(2,1)} %hid_hbm.1, bf16[2048,128]{1,0:T(8,128)(2,1)} %w_hbm.1, ...), custom_call_target="tpu_custom_call" | custom-call | tf_op jit(solution)/shard_map/pallas_call | solution.py:595
  33.1 1.8 %shard_map.87 = (bf16[256,1024]{1,0:T(8,128)(2,1)}, bf16[256,256]{1,0:T(8,128)(2,1)}) custom-call(bf16[8,256,1280]{2,1,0:T(8,128)(2,1)S(1)} %get-tuple-element.7.probs, f32[2,8,256,1]{3,2,1,0:T(8,128)S(1)} %get-tuple-element.8.tops, f32[8,256,256]{2,1,0:T(8,128)S(1)} %get-tuple-element.9.base, bf16[1024,128]{1,0:T(8,128)(2,1)S(1)} %get-tuple-element.10.near, ...), custom_call_target="tpu_custom_call" | custom-call | tf_op jit(solution)/shard_map/pallas_call | solution.py:644

commit v5 on v4

--- a/solution.py
+++ b/solution.py
@@ -441,12 +441,14 @@
             tops[part, h] = top
             probs[h, :, first:last] = weights.astype(jnp.bfloat16)
 
-        def couple(i, carry):
-            one(2 * i)
-            one(2 * i + 1)
+        some = 4 if (upper - lower) % 4 == 0 else 2
+
+        def several(i, carry):
+            for at in range(some):
+                one(lower + some * i + at)
             return carry
 
-        lax.fori_loop(lower // 2, upper // 2, couple, 0)
+        lax.fori_loop(0, (upper - lower) // some, several, 0)
 
     def mix_own(first):
         cache_ref[:, :head] = kv_ref[0, here, :]
@@ -456,12 +458,8 @@
             [kv_ref[1, rows, :], jnp.ones((width - first, head), jnp.bfloat16)], axis=1
         )
 
-        def couple(i, carry):
-            for h in (2 * i, 2 * i + 1):
-                base[h] = jnp.dot(probs[h, :, first:], values, preferred_element_type=jnp.float32)
-            return carry
-
-        lax.fori_loop(0, group // 2, couple, 0)
+        for h in range(group):
+            base[h] = jnp.dot(probs[h, :, first:], values, preferred_element_type=jnp.float32)
 
     group = q_ref.shape[1] // head
     early = group // 4 * 2
@@ -484,21 +482,34 @@
         split = halo - toks
         await_crossed([0])
         weigh(0, split, width, 0, group)
-        is_last = (neighbour(n_tp - 1) == t) & (pair != back)
-
-        @pl.when(is_last)
-        def _():
+        is_last = neighbour(n_tp - 1) == t
+        is_early = is_last & (pair != back)
+        is_end = pair == pairs - 1
+
+        def late_order(ahead):
             await_crossed(range(1, back + 1))
-            weigh(1, 0, split, 0, early)
+            weigh(1, 0, split, 0, ahead)
             finish(False)
-            weigh(1, 0, split, early, group)
+            weigh(1, 0, split, ahead, group)
             pass_on()
             mix_own(split)
 
-        @pl.when(jnp.logical_not(is_last))
+        @pl.when(is_early & jnp.logical_not(is_end))
+        def _():
+            late_order(early)
+
+        @pl.when(is_early & is_end)
+        def _():
+            late_order(most)
+
+        @pl.when(jnp.logical_not(is_early))
         def _():
             finish(False)
-            mix_own(split)
+
+            @pl.when(jnp.logical_not(is_last))
+            def _():
+                mix_own(split)
+
             await_crossed(range(1, back + 1))
             weigh(1, 0, split, 0, most)
 
@@ -511,6 +522,10 @@
             @pl.when(waits_long)
             def _():
                 pass_on()
+
+            @pl.when(is_last)
+            def _():
+                mix_own(split)
 
     near[...] = kv_ref[1, pl.ds(start, halo), :]
 

time: 35.2 us -> 35 us (level)
  no operation moved by 1% of the time
where the time goes in v5:
time: 35 us; the launch traced here: 34.9 us
  Pallas kernels  33.6 us (96%)
  between operations  1.29 us (4%)
    pallas_call x1, Pallas kernels, fast_body(): pl.pallas_call(functools.partial(fused_kernel, halo, back), out_shape=(pl...  31.8 us
    pallas_call x1, Pallas kernels, fast_body(): pl.pallas_call(mix_kernel, out_shape=(jax.ShapeDtypeStruct(queries.shape,...  1.84 us

profile of v5, /device:TPU:5, one launch (start us, length us, event | category | flops | bytes accessed | tf_op | source)
XLA Modules:
  0.0 34.9 jit_solution(5600343125607930261)
XLA Ops:
  1.3 31.8 %shard_map.86 = (bf16[8,256,1280]{2,1,0:T(8,128)(2,1)S(1)}, f32[2,8,256,1]{3,2,1,0:T(8,128)S(1)}, f32[8,256,256]{2,1,0:T(8,128)S(1)}, bf16[1024,128]{1,0:T(8,128)(2,1)S(1)}, bf16[256,256]{1,0:T(8,128)(2,1)S(1)}) custom-call(s32[1]{0:T(128)S(6)} %copy.9.window_ref, bf16[256,2048]{1,0:T(8,128)(2,1)} %hid_hbm.1, bf16[2048,128]{1,0:T(8,128)(2,1)} %w_hbm.1, ...), custom_call_target="tpu_custom_call" | custom-call | tf_op jit(solution)/shard_map/pallas_call | solution.py:610
  33.1 1.8 %shard_map.87 = (bf16[256,1024]{1,0:T(8,128)(2,1)}, bf16[256,256]{1,0:T(8,128)(2,1)}) custom-call(bf16[8,256,1280]{2,1,0:T(8,128)(2,1)S(1)} %get-tuple-element.7.probs, f32[2,8,256,1]{3,2,1,0:T(8,128)S(1)} %get-tuple-element.8.tops, f32[8,256,256]{2,1,0:T(8,128)S(1)} %get-tuple-element.9.base, bf16[1024,128]{1,0:T(8,128)(2,1)S(1)} %get-tuple-element.10.near, ...), custom_call_target="tpu_custom_call" | custom-call | tf_op jit(solution)/shard_map/pallas_call | solution.py:659
